TPU v7x, 32 devices: a whole 2x2x4 slice. The times are simulated.
32 devices in a mesh: pert: 2 (over x), ga: 16 (over z, y, core).
Axes of the slice: x: 2, y: 2, z: 4, core: 2. Of those that a mesh axis runs over, the one named last changes fastest.
Arguments:
- psi_k: bfloat16 [2, 8192, 256], P(None, 'ga'), may hold values from -6 to 6
- beta_k: bfloat16 [2, 8192, 2496], P(None, 'ga'), may hold values from -0.0625 to 0.0625
- beta_kq: bfloat16 [2, 8192, 2496], P(None, 'ga'), may hold values from -0.15625 to 0.15625
- g_k: float32 [3, 8192], P(None, 'ga'), may hold values from -2 to 2
- g_kq: float32 [3, 8192], P(None, 'ga'), may hold values from -2 to 2
- send_index: int32 [16, 16, 32], P('ga'), may hold values from -1 to 511, as said below
- recv_index: int32 [8192], P('ga'), may hold values from -1 to 511, as said below
- dmat: float32 [192, 13, 13], replicated, may hold values from -0.5 to 4, as said below
- displaced: int32 [256], P('pert'), parts along dimension 0, may hold values from 0 to 191, as said below
- mode: float32 [3, 256], P(None, 'pert'), parts along dimension 1, may hold values from -5 to 5
Outputs:
- dvpsi: bfloat16 [4, 8192, 256], P('pert', 'ga'), parts along dimension 0
There are 2 independent parts, one for each index of `pert`. A program takes and returns all parts, laid end to end along the dimension named above; an argument that names none is the same for every part. Nothing has to cross between parts.
Inputs may be any that keep to these rules, and one draw needn't show every extreme that they name: `send_index`: entry [s, d, c] is a row of device s's k-sphere block in local numbering, or -1 for an unused slot; the rows device s sends are distinct; in every draw some device receives 32 rows from every device. `recv_index`: entry r is s * 32 + c, naming slot c from device s among the rows received by the device of row r, or -1 for a row with no k-sphere counterpart; every used slot is named by exactly one row of its receiving device and no unused slot is named. `dmat`: each atom's block is symmetric. `displaced`: 128 distinct atoms.
All inputs are finite; a program needn't handle non-finite values.
Results may differ from a plain program's by a relative error of at most 0.0057.
Values may be sent and summed in bfloat16 or wider, within the bound.
No kernel may reach another device: no remote copies, remote signals or barrier semaphores. Data moves between devices by JAX's collectives and lax.ppermute only.
A program may use at most 128 MiB of HBM per device.

v0:
```python
import functools

import jax
import jax.numpy as jnp
import numpy as np
from jax import lax
from jax.experimental import pallas as pl
from jax.experimental.pallas import tpu as pltpu
from jax.sharding import PartitionSpec as P

F32, BF16 = jnp.float32, jnp.bfloat16
LANES = 128
SMEM = pl.BlockSpec(memory_space=pltpu.SMEM)


def stage_bits(count):
    first = list(range(count))
    second = list(first)
    if count > 2:
        second[1], second[2] = 2, 1
    return first, second


def block_order(bits):
    count = len(bits)
    return [
        sum(((place >> (count - 1 - i)) & 1) << bits[i] for i in range(count))
        for place in range(1 << count)
    ]


def cost(flops, moved):
    return pl.CostEstimate(flops=flops, bytes_accessed=moved, transcendentals=0)


def pack_kernel(slot_ref, psi_ref, out_ref):
    rows, slots = psi_ref.shape[1], slot_ref.shape[1]
    chosen = lax.broadcasted_iota(jnp.int32, (rows, slots), 0) == slot_ref[...]
    chosen = chosen.astype(BF16)
    bands = psi_ref.shape[2]
    for part in range(2):
        rows_out = lax.dot_general(
            chosen, psi_ref[part], (((0,), (0,)), ((), ())), preferred_element_type=F32
        )
        out_ref[:, part * bands : (part + 1) * bands] = rows_out.astype(BF16)


def pack_rows(slots, psi):
    count = slots.shape[1]
    return pl.pallas_call(
        pack_kernel,
        out_shape=jax.ShapeDtypeStruct((count, 2 * psi.shape[2]), BF16),
        cost_estimate=cost(2 * count * psi.shape[1] * 512, 2_000_000),
    )(slots, psi)


def place_kernel(recv_ref, out_ref):
    chosen = lax.broadcasted_iota(jnp.int32, out_ref.shape, 0) == recv_ref[...]
    out_ref[...] = chosen.astype(F32).T.astype(BF16)


def place_matrix(recv, slots):
    return pl.pallas_call(
        place_kernel, out_shape=jax.ShapeDtypeStruct((recv.shape[1], slots), BF16)
    )(recv)


def widen_rows(source, wide):
    rows, step = source.shape[1], 96
    while rows % step:
        step -= 8

    def body(index, carry):
        start = pl.multiple_of(index * step, 8)
        for l in range(wide.shape[0]):
            lanes = slice(LANES * l, LANES * (l + 1))
            wide[l, pl.ds(start, step), :] = source[0, pl.ds(start, step), lanes].astype(F32)
        return carry

    lax.fori_loop(0, rows // step, body, 0)


def walk_atoms(wide, tables, vectors, place, atoms, size, store):
    home, order, displaced, mode = tables
    base = (home[0] ^ order[place]) * atoms
    for i in range(atoms):
        start = displaced[base + i] * size
        amount = [mode[x, base + i] for x in range(3)]
        for l in range(wide.shape[0]):
            lanes = slice(LANES * l, LANES * (l + 1))
            picked = wide[l, pl.ds(start, size), :]
            weight = (
                amount[0] * vectors[0:1, lanes]
                + amount[1] * vectors[1:2, lanes]
                + amount[2] * vectors[2:3, lanes]
            )
            store(i, l, picked, weight)


def bra_kernel(atoms, size, home, order, swap, displaced, mode, source, vectors, *rest):
    plain, scaled, wide, slab, slab_scaled = rest[0:2], rest[2:4], rest[4], rest[5], rest[6]
    half, block = plain[0].shape[1:3]
    widen_rows(source, wide)
    if block != atoms * size:
        slab[...] = jnp.zeros_like(slab)
        slab_scaled[...] = jnp.zeros_like(slab_scaled)

    def store(i, l, picked, weight):
        slab[l, size * i : size * (i + 1), :] = picked
        slab_scaled[l, size * i : size * (i + 1), :] = picked * weight

    for h in range(2):

        def body(index, carry):
            place = h * half + index
            walk_atoms(
                wide, (home, order, displaced, mode), vectors, place, atoms, size, store
            )
            other = swap[place] - h * half
            for l in range(wide.shape[0]):
                lanes = slice(LANES * l, LANES * (l + 1))
                plain[h][0, index, :, lanes] = slab[l].astype(BF16)
                scaled[h][0, other, :, lanes] = slab_scaled[l].astype(BF16)
            return carry

        lax.fori_loop(0, half, body, 0)


def ket_kernel(atoms, size, block, home, order, swap, displaced, mode, source, vectors, *rest):
    turned, wide, slab = rest[0:2], rest[2], rest[3]
    half = slab.shape[1] // (2 * block)
    widen_rows(source, wide)
    if block != atoms * size:
        slab[...] = jnp.zeros_like(slab)
    for h in range(2):

        def body(index, carry):
            place = h * half + index
            plain_row = pl.multiple_of((swap[place] - h * half) * block, 8)
            scaled_row = pl.multiple_of((half + index) * block, 8)

            def store(i, l, picked, weight):
                slab[l, pl.ds(plain_row + size * i, size), :] = picked
                slab[l, pl.ds(scaled_row + size * i, size), :] = -(picked * weight)

            walk_atoms(
                wide, (home, order, displaced, mode), vectors, place, atoms, size, store
            )
            return carry

        lax.fori_loop(0, half, body, 0)
        for j in range(slab.shape[1] // LANES):
            for l in range(wide.shape[0]):
                chunk = slab[l, LANES * j : LANES * (j + 1), :]
                turned[h][0, LANES * l : LANES * (l + 1), LANES * j : LANES * (j + 1)] = (
                    chunk.T.astype(BF16)
                )


def prepare_bra(tables, beta, vectors, atoms, size, block):
    half = tables[1].shape[0] // 2
    rows, width = beta.shape[1:]
    out = jax.ShapeDtypeStruct((2, half, block, width), BF16)
    return pl.pallas_call(
        functools.partial(bra_kernel, atoms, size),
        grid=(2,),
        in_specs=[SMEM] * 5
        + [
            pl.BlockSpec((1, rows, width), lambda c: (c, 0, 0)),
            pl.BlockSpec(vectors.shape, lambda c: (0, 0)),
        ],
        out_specs=[pl.BlockSpec((1, half, block, width), lambda c: (c, 0, 0, 0))] * 4,
        out_shape=[out] * 4,
        scratch_shapes=[
            pltpu.VMEM((width // LANES, rows, LANES), F32),
            pltpu.VMEM((width // LANES, block, LANES), F32),
            pltpu.VMEM((width // LANES, block, LANES), F32),
        ],
        cost_estimate=cost(8_000_000_000, 12_000_000),
    )(*tables, beta, vectors)


def prepare_ket(tables, beta, vectors, atoms, size, block):
    half = tables[1].shape[0] // 2
    rows, width = beta.shape[1:]
    out = jax.ShapeDtypeStruct((2, width, 2 * half * block), BF16)
    return pl.pallas_call(
        functools.partial(ket_kernel, atoms, size, block),
        grid=(2,),
        in_specs=[SMEM] * 5
        + [
            pl.BlockSpec((1, rows, width), lambda c: (c, 0, 0)),
            pl.BlockSpec(vectors.shape, lambda c: (0, 0)),
        ],
        out_specs=[pl.BlockSpec((1, width, 2 * half * block), lambda c: (c, 0, 0))] * 2,
        out_shape=[out] * 2,
        scratch_shapes=[
            pltpu.VMEM((width // LANES, rows, LANES), F32),
            pltpu.VMEM((width // LANES, 2 * half * block, LANES), F32),
        ],
        cost_estimate=cost(8_000_000_000, 12_000_000),
    )(*tables, beta, vectors)


def wave_kernel(arrived_ref, place_ref, left_ref, waves_ref, out_ref):
    bands = arrived_ref.shape[1] // 2
    rows = jnp.dot(place_ref[...], arrived_ref[...], preferred_element_type=F32).astype(BF16)
    waves_ref[0] = rows
    waves_ref[1, :, :bands] = rows[:, bands:]
    waves_ref[1, :, bands:] = -rows[:, :bands]
    project_kernel(waves_ref, left_ref, out_ref)


def project_kernel(waves_ref, left_ref, out_ref):
    total = jnp.dot(left_ref[0], waves_ref[0], preferred_element_type=F32)
    total += jnp.dot(left_ref[1], waves_ref[1], preferred_element_type=F32)
    out_ref[...] = total.astype(out_ref.dtype)


def first_project(arrived, place, left):
    rows, width = arrived.shape
    return pl.pallas_call(
        wave_kernel,
        out_shape=(
            jax.ShapeDtypeStruct((2, place.shape[0], width), BF16),
            jax.ShapeDtypeStruct((left.shape[1], width), BF16),
        ),
        cost_estimate=cost(4 * left.shape[1] * rows * width, 4_000_000),
    )(arrived, place, left)


def project(waves, left, kind):
    return pl.pallas_call(
        project_kernel,
        out_shape=jax.ShapeDtypeStruct((left.shape[1], waves.shape[2]), kind),
        cost_estimate=cost(4 * left.shape[1] * waves.shape[1] * waves.shape[2], 4_000_000),
    )(waves, left)


def couple_kernel(matrix_ref, *refs):
    for kept, came, out in zip(refs[0:2], refs[2:4], refs[4:6]):
        total = kept[...] + came[...].astype(F32)
        out[...] = jnp.dot(
            matrix_ref[...],
            total,
            precision=lax.Precision.HIGHEST,
            preferred_element_type=F32,
        ).astype(BF16)


def couple(matrix, kept, came):
    out = jax.ShapeDtypeStruct(kept[0].shape, BF16)
    return pl.pallas_call(
        couple_kernel,
        out_shape=(out, out),
        cost_estimate=cost(200_000_000, 1_000_000),
    )(matrix, *kept, *came)


def back_first_kernel(left_ref, z_ref, x_ref, out_ref):
    right = jnp.concatenate([z_ref[...], x_ref[...]], axis=0)
    for part in range(2):
        out_ref[part] = jnp.dot(left_ref[part], right, preferred_element_type=F32)


def back_last_kernel(left_ref, z_ref, x_ref, start_ref, out_ref):
    right = jnp.concatenate([z_ref[...], x_ref[...]], axis=0)
    bands = out_ref.shape[2]
    real, imag = (
        start_ref[part] + jnp.dot(left_ref[part], right, preferred_element_type=F32)
        for part in range(2)
    )
    out_ref[0] = (-(real[:, bands:] + imag[:, :bands])).astype(BF16)
    out_ref[1] = (real[:, :bands] - imag[:, bands:]).astype(BF16)


def back_first(left, z, x):
    return pl.pallas_call(
        back_first_kernel,
        out_shape=jax.ShapeDtypeStruct((2, left.shape[1], z.shape[1]), F32),
        cost_estimate=cost(4 * left.shape[1] * left.shape[2] * z.shape[1], 6_000_000),
    )(left, z, x)


def back_last(left, z, x, start):
    return pl.pallas_call(
        back_last_kernel,
        out_shape=jax.ShapeDtypeStruct((2, left.shape[1], z.shape[1] // 2), BF16),
        cost_estimate=cost(4 * left.shape[1] * left.shape[2] * z.shape[1], 6_000_000),
    )(left, z, x, start)


def trade(value, bit):
    members = lax.axis_size("ga")
    return lax.ppermute(value, "ga", [(i, i ^ (1 << bit)) for i in range(members)])


def on_device(psi_k, beta_k, beta_kq, g_k, g_kq, send_index, recv_index, dmat, displaced, mode):
    groups = lax.axis_size("ga")
    count = groups.bit_length() - 1
    capacity = send_index.shape[2]
    slots = groups * capacity
    size = dmat.shape[1]
    atoms = displaced.shape[0] // groups
    block = -(-atoms * size // 8) * 8
    if block * groups % LANES:
        block = -(-block // 16) * 16
    me = lax.axis_index("ga").astype(jnp.int32)
    streams = stage_bits(count)
    orders = [block_order(bits) for bits in streams]
    swap = np.array([orders[1].index(k) for k in orders[0]], np.int32)
    tables = (
        me.reshape(1),
        jnp.asarray(np.array(orders[0], np.int32)),
        jnp.asarray(swap),
        displaced,
        mode,
    )

    packed = pack_rows(send_index.reshape(1, slots), psi_k)
    arrived = lax.all_to_all(
        packed.reshape(groups, capacity, -1), "ga", split_axis=0, concat_axis=0, tiled=True
    ).reshape(slots, -1)
    place = place_matrix(recv_index.reshape(1, -1), slots)
    lefts = prepare_bra(tables, jnp.swapaxes(beta_k, 1, 2), g_k, atoms, size, block)
    lefts = [left.reshape(2, -1, left.shape[3]) for left in lefts]

    own = lax.dynamic_slice_in_dim(displaced, me * atoms, atoms)
    coupling = jnp.take(dmat, own, axis=0)
    matrix = (jnp.eye(atoms, dtype=F32)[:, None, :, None] * coupling[:, :, None, :]).reshape(
        atoms * size, atoms * size
    )
    spare = block - atoms * size
    matrix = jnp.pad(matrix, ((0, spare), (0, spare)))

    waves, away_first = first_project(arrived, place, lefts[1])
    came_first = trade(away_first, streams[0][0])
    away_second = project(waves, lefts[3], BF16)
    came_second = trade(away_second, streams[1][0])
    kept = [project(waves, lefts[0], F32), project(waves, lefts[2], F32)]
    came = [came_first, came_second]

    for stage in range(1, count):
        away = []
        for s in range(2):
            total = (kept[s] + came[s].astype(F32)).reshape(2, -1, kept[s].shape[1])
            kept[s] = total[0]
            away.append(total[1].astype(BF16))
        came = [trade(away[s], streams[s][stage]) for s in range(2)]

    gathered = list(couple(matrix, kept, came))
    turned = prepare_ket(tables, jnp.swapaxes(beta_kq, 1, 2), g_kq, atoms, size, block)
    for stage in range(count - 1, 0, -1):
        came = [trade(gathered[s], streams[s][stage]) for s in range(2)]
        gathered = [jnp.concatenate([gathered[s], came[s]], axis=0) for s in range(2)]
    came = [trade(gathered[s], streams[s][0]) for s in range(2)]
    start = back_first(turned[0], gathered[1], gathered[0])
    return back_last(turned[1], came[1], came[0], start)


def solution(mesh):
    in_specs = (
        P(None, "ga", None),
        P(None, "ga", None),
        P(None, "ga", None),
        P(None, "ga"),
        P(None, "ga"),
        P("ga", None, None),
        P("ga"),
        P(),
        P("pert"),
        P(None, "pert"),
    )
    out_specs = P("pert", "ga", None)
    return jax.shard_map(
        on_device, mesh=mesh, in_specs=in_specs, out_specs=out_specs, check_vma=False
    )
```

profile of v0, /device:TPU:0, one launch (start us, length us, event | category | flops | bytes accessed | tf_op | source)
XLA Modules:
  0.0 131.0 jit_solution(8521031212758875788)
XLA Ops:
  1.4 2.3 %shard_map.119 = bf16[512,512]{1,0:T(8,128)(2,1)} custom-call(s32[1,512]{1,0:T(1,128)} %reshape.78.slot_ref, bf16[2,512,256]{2,1,0:T(8,128)(2,1)} %psi_ref.1), custom_call_target="tpu_custom_call" | custom-call | flops 268435456 | bytes 2000000 | tf_op jit(solution)/shard_map/pallas_call | solution.py:50
  3.7 7.4 %all-to-all-start = ((bf16[16,32,512]{2,1,0:T(8,128)(2,1)}), bf16[16,32,512]{2,1,0:T(8,128)(2,1)S(1)}, u32[]{:S(2)}, u32[]{:S(2)}) async-start(bf16[16,32,512]{2,1,0:T(8,128)(2,1)} %bitcast.12), calls=%async_computation | async-start | bytes 1048576 | tf_op jit(solution)/shard_map/all_to_all | solution.py:321
  11.1 1.7 %shard_map.120.place_ref = bf16[512,512]{1,0:T(8,128)(2,1)} custom-call(s32[1,512]{1,0:T(1,128)} %bitcast.17), custom_call_target="tpu_custom_call" | custom-call | tf_op jit(solution)/shard_map/pallas_call | solution.py:63
  12.8 7.2 %shard_map.121 = (bf16[2,8,104,512]{3,2,1,0:T(8,128)(2,1)}, bf16[2,8,104,512]{3,2,1,0:T(8,128)(2,1)}, bf16[2,8,104,512]{3,2,1,0:T(8,128)(2,1)}, bf16[2,8,104,512]{3,2,1,0:T(8,128)(2,1)}) custom-call(s32[1]{0:T(128)} %bitcast.home, s32[16]{0:T(128)} %constant.29.clone.order, s32[16]{0:T(128)} %constant.30.clone.swap, s32[128]{0:T(128)} %displaced.3, ...), custom_call_target="tpu_custom_call" | custom-call | flops 8000000000 | bytes 12000000 | tf_op jit(solution)/shard_map/pallas_call | solution.py:164
  20.0 5.4 %all-to-all-done = bf16[16,32,512]{2,1,0:T(8,128)(2,1)S(1)} async-done(((bf16[16,32,512]{2,1,0:T(8,128)(2,1)}), bf16[16,32,512]{2,1,0:T(8,128)(2,1)S(1)}, u32[]{:S(2)}, u32[]{:S(2)}) %all-to-all-start) | async-done | bytes 524320 | tf_op jit(solution)/shard_map/all_to_all | solution.py:321
  26.2 4.1 %shard_map.122 = (bf16[2,512,512]{2,1,0:T(8,128)(2,1)}, bf16[832,512]{1,0:T(8,128)(2,1)}) custom-call(bf16[512,512]{1,0:T(8,128)(2,1)} %bitcast.16, bf16[512,512]{1,0:T(8,128)(2,1)} %shard_map.120.place_ref, bf16[2,832,512]{2,1,0:T(8,128)(2,1)} %bitcast.20), custom_call_target="tpu_custom_call" | custom-call | flops 872415232 | bytes 4000000 | tf_op jit(solution)/shard_map/pallas_call | solution.py:222
  30.3 3.8 %shard_map.125 = bf16[832,512]{1,0:T(8,128)(2,1)} custom-call(bf16[2,512,512]{2,1,0:T(8,128)(2,1)} %get-tuple-element.17.waves_ref, bf16[2,832,512]{2,1,0:T(8,128)(2,1)} %bitcast.13), custom_call_target="tpu_custom_call" | custom-call | flops 872415232 | bytes 4000000 | tf_op jit(solution)/shard_map/pallas_call | solution.py:233
  36.1 4.1 %shard_map.124 = f32[832,512]{1,0:T(8,128)} custom-call(bf16[2,512,512]{2,1,0:T(8,128)(2,1)} %get-tuple-element.17.waves_ref, bf16[2,832,512]{2,1,0:T(8,128)(2,1)} %bitcast.15), custom_call_target="tpu_custom_call" | custom-call | flops 872415232 | bytes 4000000 | tf_op jit(solution)/shard_map/pallas_call | solution.py:233
  40.2 4.1 %shard_map.123 = f32[832,512]{1,0:T(8,128)} custom-call(bf16[2,512,512]{2,1,0:T(8,128)(2,1)} %get-tuple-element.17.waves_ref, bf16[2,832,512]{2,1,0:T(8,128)(2,1)} %bitcast.14), custom_call_target="tpu_custom_call" | custom-call | flops 872415232 | bytes 4000000 | tf_op jit(solution)/shard_map/pallas_call | solution.py:233
  47.7 8.9 %collective-permute-done.4 = bf16[416,512]{1,0:T(8,128)(2,1)S(1)} collective-permute-done((bf16[416,512]{1,0:T(8,128)(2,1)S(1)}, bf16[416,512]{1,0:T(8,128)(2,1)S(1)}, u32[]{:S(2)}, u32[]{:S(2)}) %collective-permute-start.4) | collective-permute-done | bytes 426016 | tf_op jit(solution)/shard_map/ppermute | solution.py:295
  60.1 3.2 %collective-permute-done.5 = bf16[208,512]{1,0:T(8,128)(2,1)S(1)} collective-permute-done((bf16[208,512]{1,0:T(8,128)(2,1)S(1)}, bf16[208,512]{1,0:T(8,128)(2,1)S(1)}, u32[]{:S(2)}, u32[]{:S(2)}) %collective-permute-start.5) | collective-permute-done | bytes 213024 | tf_op jit(solution)/shard_map/ppermute | solution.py:295
  63.4 2.2 %collective-permute-start.7 = (bf16[104,512]{1,0:T(8,128)(2,1)S(1)}, bf16[104,512]{1,0:T(8,128)(2,1)S(1)}, u32[]{:S(2)}, u32[]{:S(2)}) collective-permute-start(bf16[104,512]{1,0:T(8,128)(2,1)S(1)} %slice.94), channel_id=1, source_target_pairs={{0,8},{1,9},{2,10},{3,11},{4,12},{5,13},{6,14},{7,15},{8,0},{9,1},... | collective-permute-start | bytes 319496 | tf_op jit(solution)/shard_map/ppermute | solution.py:295
  69.3 4.8 %collective-permute-done.7.refs_3_ = bf16[104,512]{1,0:T(8,128)(2,1)S(1)} collective-permute-done((bf16[104,512]{1,0:T(8,128)(2,1)S(1)}, bf16[104,512]{1,0:T(8,128)(2,1)S(1)}, u32[]{:S(2)}, u32[]{:S(2)}) %collective-permute-start.7) | collective-permute-done | bytes 106528 | tf_op jit(solution)/shard_map/ppermute | solution.py:295
  75.9 2.3 %shard_map.126 = (bf16[104,512]{1,0:T(8,128)(2,1)}, bf16[104,512]{1,0:T(8,128)(2,1)}) custom-call(f32[104,104]{1,0:T(8,128)} %mul.24.matrix_ref, f32[104,512]{1,0:T(8,128)} %slice.72.refs_0_, f32[104,512]{1,0:T(8,128)} %slice.77.refs_1_, bf16[104,512]{1,0:T(8,128)(2,1)} %copy-done.11, bf16[104,512]{1,0:T(8,128)(2,1)} %copy-done.10), custom_call_target="tpu_custom_call" | custom-call | flops 200000000 | bytes 1000000 | tf_op jit(solution)/shard_map/pallas_call | solution.py:253
  78.3 2.9 %collective-permute-start.8 = (bf16[104,512]{1,0:T(8,128)(2,1)}, bf16[104,512]{1,0:T(8,128)(2,1)S(1)}, u32[]{:S(2)}, u32[]{:S(2)}) collective-permute-start(bf16[104,512]{1,0:T(8,128)(2,1)} %get-tuple-element.22), channel_id=1, source_target_pairs={{0,8},{1,9},{2,10},{3,11},{4,12},{5,13},{6,14},{7,15},{8,0},{9,1},... | collective-permute-start | bytes 319496 | tf_op jit(solution)/shard_map/ppermute | solution.py:295
  82.1 5.2 %collective-permute-done.12 = bf16[104,512]{1,0:T(8,128)(2,1)S(1)} collective-permute-done((bf16[104,512]{1,0:T(8,128)(2,1)}, bf16[104,512]{1,0:T(8,128)(2,1)S(1)}, u32[]{:S(2)}, u32[]{:S(2)}) %collective-permute-start.12) | collective-permute-done | bytes 106528 | tf_op jit(solution)/shard_map/ppermute | solution.py:295
  90.1 2.3 %collective-permute-start.9 = (bf16[208,512]{1,0:T(8,128)(2,1)S(1)}, bf16[208,512]{1,0:T(8,128)(2,1)S(1)}, u32[]{:S(2)}, u32[]{:S(2)}) collective-permute-start(bf16[208,512]{1,0:T(8,128)(2,1)S(1)} %pad_maximum_fusion.2), channel_id=1, source_target_pairs={{0,2},{1,3},{2,0},{3,1},{4,6},{5,7},{6,4},{7,5},{8,10},{9,11},{10,... | collective-permute-start | bytes 638984 | tf_op jit(solution)/shard_map/ppermute | solution.py:295
  92.4 2.3 %collective-permute-done.13 = bf16[208,512]{1,0:T(8,128)(2,1)S(1)} collective-permute-done((bf16[208,512]{1,0:T(8,128)(2,1)S(1)}, bf16[208,512]{1,0:T(8,128)(2,1)S(1)}, u32[]{:S(2)}, u32[]{:S(2)}) %collective-permute-start.13) | collective-permute-done | bytes 213024 | tf_op jit(solution)/shard_map/ppermute | solution.py:295
  95.6 2.7 %collective-permute-start.14 = (bf16[416,512]{1,0:T(8,128)(2,1)S(1)}, bf16[416,512]{1,0:T(8,128)(2,1)S(1)}, u32[]{:S(2)}, u32[]{:S(2)}) collective-permute-start(bf16[416,512]{1,0:T(8,128)(2,1)S(1)} %pad_maximum_fusion.1), channel_id=1, source_target_pairs={{0,2},{1,3},{2,0},{3,1},{4,6},{5,7},{6,4},{7,5},{8,10},{9,11},{10,... | collective-permute-start | bytes 1277960 | tf_op jit(solution)/shard_map/ppermute | solution.py:295
  98.7 8.6 %collective-permute-done.14 = bf16[416,512]{1,0:T(8,128)(2,1)S(1)} collective-permute-done((bf16[416,512]{1,0:T(8,128)(2,1)S(1)}, bf16[416,512]{1,0:T(8,128)(2,1)S(1)}, u32[]{:S(2)}, u32[]{:S(2)}) %collective-permute-start.14) | collective-permute-done | bytes 426016 | tf_op jit(solution)/shard_map/ppermute | solution.py:295
  107.4 1.6 %collective-permute-done.10 = bf16[416,512]{1,0:T(8,128)(2,1)S(1)} collective-permute-done((bf16[416,512]{1,0:T(8,128)(2,1)S(1)}, bf16[416,512]{1,0:T(8,128)(2,1)S(1)}, u32[]{:S(2)}, u32[]{:S(2)}) %collective-permute-start.10) | collective-permute-done | bytes 426016 | tf_op jit(solution)/shard_map/ppermute | solution.py:295
  109.2 8.6 %shard_map.118 = (bf16[2,512,1664]{2,1,0:T(8,128)(2,1)}, bf16[2,512,1664]{2,1,0:T(8,128)(2,1)}) custom-call(s32[1]{0:T(128)} %bitcast.home, s32[16]{0:T(128)} %constant.29.clone.order, s32[16]{0:T(128)} %constant.30.clone.swap, s32[128]{0:T(128)} %displaced.3, f32[3,128]{1,0:T(4,128)} %mode.3, bf16[2,2496,512]{2,1,0:T(8,128)(2,1)} %bitcast.19, f32[3,512]{1,0:T(4,128)} %vectors.2), custom_call_target="tpu_custom_call" | custom-call | flops 8000000000 | bytes 12000000 | tf_op jit(solution)/shard_map/pallas_call | solution.py:187
  117.8 5.9 %shard_map.127.start_ref = f32[2,512,512]{2,1,0:T(8,128)} custom-call(bf16[2,512,1664]{2,1,0:T(8,128)(2,1)} %get-tuple-element.24.left_ref, bf16[832,512]{1,0:T(8,128)(2,1)} %copy-done.2, bf16[832,512]{1,0:T(8,128)(2,1)} %copy-done.3), custom_call_target="tpu_custom_call" | custom-call | flops 1744830464 | bytes 6000000 | tf_op jit(solution)/shard_map/pallas_call | solution.py:278
  125.0 6.0 %shard_map.128 = bf16[2,512,256]{2,1,0:T(8,128)(2,1)} custom-call(bf16[2,512,1664]{2,1,0:T(8,128)(2,1)} %get-tuple-element.15.left_ref, bf16[832,512]{1,0:T(8,128)(2,1)} %copy-done.6, bf16[832,512]{1,0:T(8,128)(2,1)} %copy-done.5, f32[2,512,512]{2,1,0:T(8,128)} %shard_map.127.start_ref), custom_call_target="tpu_custom_call" | custom-call | flops 1744830464 | bytes 6000000 | tf_op jit(solution)/shard_map/pallas_call | solution.py:286
  (79 shorter events, 23.0 us)
Async XLA Ops:
  3.7 21.7 %all-to-all-start = ((bf16[16,32,512]{2,1,0:T(8,128)(2,1)}), bf16[16,32,512]{2,1,0:T(8,128)(2,1)S(1)}, u32[]{:S(2)}, u32[]{:S(2)}) async-start(bf16[16,32,512]{2,1,0:T(8,128)(2,1)} %bitcast.12), calls=%async_computation | async-start | bytes 1048576 | tf_op jit(solution)/shard_map/all_to_all | solution.py:321
  30.3 4.3 %copy-start.8 = (f32[192,13,13]{0,2,1:T(8,128)S(1)}, f32[192,13,13]{0,2,1:T(8,128)}, u32[]{:S(2)}) copy-start(f32[192,13,13]{0,2,1:T(8,128)} %param.19) | copy-start | bytes 389380
  34.1 1.4 %copy-start.9 = (s32[128]{0:T(128)S(1)}, s32[128]{0:T(128)}, u32[]{:S(2)}) copy-start(s32[128]{0:T(128)} %displaced.3) | copy-start | bytes 1540
  34.1 10.3 %collective-permute-start.3 = (bf16[832,512]{1,0:T(8,128)(2,1)}, bf16[832,512]{1,0:T(8,128)(2,1)S(1)}, u32[]{:S(2)}, u32[]{:S(2)}) collective-permute-start(bf16[832,512]{1,0:T(8,128)(2,1)} %shard_map.125), channel_id=1, source_target_pairs={{0,1},{1,0},{2,3},{3,2},{4,5},{5,4},{6,7},{7,6},{8,9},{9,8},{10,11... | collective-permute-start | bytes 2555912 | tf_op jit(solution)/shard_map/ppermute | solution.py:295
  34.2 11.9 %collective-permute-start = (bf16[832,512]{1,0:T(8,128)(2,1)}, bf16[832,512]{1,0:T(8,128)(2,1)S(1)}, u32[]{:S(2)}, u32[]{:S(2)}) collective-permute-start(bf16[832,512]{1,0:T(8,128)(2,1)} %get-tuple-element.19), channel_id=1, source_target_pairs={{0,1},{1,0},{2,3},{3,2},{4,5},{5,4},{6,7},{7,6},{8,9},{9,8},{10,11... | collective-permute-start | bytes 2555912 | tf_op jit(solution)/shard_map/ppermute | solution.py:295
  40.2 4.1 %copy-start.1 = (f32[832,512]{1,0:T(8,128)S(1)}, f32[832,512]{1,0:T(8,128)}, u32[]{:S(2)}) copy-start(f32[832,512]{1,0:T(8,128)} %shard_map.124) | copy-start | bytes 5111812
  44.3 1.8 %copy-start = (f32[832,512]{1,0:T(8,128)S(1)}, f32[832,512]{1,0:T(8,128)}, u32[]{:S(2)}) copy-start(f32[832,512]{1,0:T(8,128)} %shard_map.123) | copy-start | bytes 5111812
  44.7 11.9 %collective-permute-start.4 = (bf16[416,512]{1,0:T(8,128)(2,1)S(1)}, bf16[416,512]{1,0:T(8,128)(2,1)S(1)}, u32[]{:S(2)}, u32[]{:S(2)}) collective-permute-start(bf16[416,512]{1,0:T(8,128)(2,1)S(1)} %slice.90), channel_id=1, source_target_pairs={{0,4},{1,5},{2,6},{3,7},{4,0},{5,1},{6,2},{7,3},{8,12},{9,13},{10,... | collective-permute-start | bytes 1277960 | tf_op jit(solution)/shard_map/ppermute | solution.py:295
  46.5 12.0 %collective-permute-start.1 = (bf16[416,512]{1,0:T(8,128)(2,1)S(1)}, bf16[416,512]{1,0:T(8,128)(2,1)S(1)}, u32[]{:S(2)}, u32[]{:S(2)}) collective-permute-start(bf16[416,512]{1,0:T(8,128)(2,1)S(1)} %slice.91), channel_id=1, source_target_pairs={{0,2},{1,3},{2,0},{3,1},{4,6},{5,7},{6,4},{7,5},{8,10},{9,11},{10,... | collective-permute-start | bytes 1277960 | tf_op jit(solution)/shard_map/ppermute | solution.py:295
  56.8 6.5 %collective-permute-start.5 = (bf16[208,512]{1,0:T(8,128)(2,1)S(1)}, bf16[208,512]{1,0:T(8,128)(2,1)S(1)}, u32[]{:S(2)}, u32[]{:S(2)}) collective-permute-start(bf16[208,512]{1,0:T(8,128)(2,1)S(1)} %slice.92), channel_id=1, source_target_pairs={{0,2},{1,3},{2,0},{3,1},{4,6},{5,7},{6,4},{7,5},{8,10},{9,11},{10,... | collective-permute-start | bytes 638984 | tf_op jit(solution)/shard_map/ppermute | solution.py:295
  58.7 6.9 %collective-permute-start.2 = (bf16[208,512]{1,0:T(8,128)(2,1)S(1)}, bf16[208,512]{1,0:T(8,128)(2,1)S(1)}, u32[]{:S(2)}, u32[]{:S(2)}) collective-permute-start(bf16[208,512]{1,0:T(8,128)(2,1)S(1)} %slice.93), channel_id=1, source_target_pairs={{0,4},{1,5},{2,6},{3,7},{4,0},{5,1},{6,2},{7,3},{8,12},{9,13},{10,... | collective-permute-start | bytes 638984 | tf_op jit(solution)/shard_map/ppermute | solution.py:295
  63.4 10.7 %collective-permute-start.7 = (bf16[104,512]{1,0:T(8,128)(2,1)S(1)}, bf16[104,512]{1,0:T(8,128)(2,1)S(1)}, u32[]{:S(2)}, u32[]{:S(2)}) collective-permute-start(bf16[104,512]{1,0:T(8,128)(2,1)S(1)} %slice.94), channel_id=1, source_target_pairs={{0,8},{1,9},{2,10},{3,11},{4,12},{5,13},{6,14},{7,15},{8,0},{9,1},... | collective-permute-start | bytes 319496 | tf_op jit(solution)/shard_map/ppermute | solution.py:295
  65.7 9.6 %collective-permute-start.6 = (bf16[104,512]{1,0:T(8,128)(2,1)S(1)}, bf16[104,512]{1,0:T(8,128)(2,1)S(1)}, u32[]{:S(2)}, u32[]{:S(2)}) collective-permute-start(bf16[104,512]{1,0:T(8,128)(2,1)S(1)} %slice.95), channel_id=1, source_target_pairs={{0,8},{1,9},{2,10},{3,11},{4,12},{5,13},{6,14},{7,15},{8,0},{9,1},... | collective-permute-start | bytes 319496 | tf_op jit(solution)/shard_map/ppermute | solution.py:295
  78.2 20.0 %copy-start.4 = (bf16[104,512]{1,0:T(8,128)(2,1)S(1)}, bf16[104,512]{1,0:T(8,128)(2,1)}, u32[]{:S(2)}) copy-start(bf16[104,512]{1,0:T(8,128)(2,1)} %get-tuple-element.22) | copy-start | bytes 319492
  78.3 9.1 %collective-permute-start.12 = (bf16[104,512]{1,0:T(8,128)(2,1)}, bf16[104,512]{1,0:T(8,128)(2,1)S(1)}, u32[]{:S(2)}, u32[]{:S(2)}) collective-permute-start(bf16[104,512]{1,0:T(8,128)(2,1)} %get-tuple-element.23), channel_id=1, source_target_pairs={{0,8},{1,9},{2,10},{3,11},{4,12},{5,13},{6,14},{7,15},{8,0},{9,1},... | collective-permute-start | bytes 319496 | tf_op jit(solution)/shard_map/ppermute | solution.py:295
  78.3 10.9 %collective-permute-start.8 = (bf16[104,512]{1,0:T(8,128)(2,1)}, bf16[104,512]{1,0:T(8,128)(2,1)S(1)}, u32[]{:S(2)}, u32[]{:S(2)}) collective-permute-start(bf16[104,512]{1,0:T(8,128)(2,1)} %get-tuple-element.22), channel_id=1, source_target_pairs={{0,8},{1,9},{2,10},{3,11},{4,12},{5,13},{6,14},{7,15},{8,0},{9,1},... | collective-permute-start | bytes 319496 | tf_op jit(solution)/shard_map/ppermute | solution.py:295
  88.2 6.4 %collective-permute-start.13 = (bf16[208,512]{1,0:T(8,128)(2,1)S(1)}, bf16[208,512]{1,0:T(8,128)(2,1)S(1)}, u32[]{:S(2)}, u32[]{:S(2)}) collective-permute-start(bf16[208,512]{1,0:T(8,128)(2,1)S(1)} %pad_maximum_fusion.3), channel_id=1, source_target_pairs={{0,4},{1,5},{2,6},{3,7},{4,0},{5,1},{6,2},{7,3},{8,12},{9,13},{10,... | collective-permute-start | bytes 638984 | tf_op jit(solution)/shard_map/ppermute | solution.py:295
  90.1 8.2 %collective-permute-start.9 = (bf16[208,512]{1,0:T(8,128)(2,1)S(1)}, bf16[208,512]{1,0:T(8,128)(2,1)S(1)}, u32[]{:S(2)}, u32[]{:S(2)}) collective-permute-start(bf16[208,512]{1,0:T(8,128)(2,1)S(1)} %pad_maximum_fusion.2), channel_id=1, source_target_pairs={{0,2},{1,3},{2,0},{3,1},{4,6},{5,7},{6,4},{7,5},{8,10},{9,11},{10,... | collective-permute-start | bytes 638984 | tf_op jit(solution)/shard_map/ppermute | solution.py:295
  95.6 11.7 %collective-permute-start.14 = (bf16[416,512]{1,0:T(8,128)(2,1)S(1)}, bf16[416,512]{1,0:T(8,128)(2,1)S(1)}, u32[]{:S(2)}, u32[]{:S(2)}) collective-permute-start(bf16[416,512]{1,0:T(8,128)(2,1)S(1)} %pad_maximum_fusion.1), channel_id=1, source_target_pairs={{0,2},{1,3},{2,0},{3,1},{4,6},{5,7},{6,4},{7,5},{8,10},{9,11},{10,... | collective-permute-start | bytes 1277960 | tf_op jit(solution)/shard_map/ppermute | solution.py:295
  98.3 10.8 %collective-permute-start.10 = (bf16[416,512]{1,0:T(8,128)(2,1)S(1)}, bf16[416,512]{1,0:T(8,128)(2,1)S(1)}, u32[]{:S(2)}, u32[]{:S(2)}) collective-permute-start(bf16[416,512]{1,0:T(8,128)(2,1)S(1)} %pad_maximum_fusion), channel_id=1, source_target_pairs={{0,4},{1,5},{2,6},{3,7},{4,0},{5,1},{6,2},{7,3},{8,12},{9,13},{10,... | collective-permute-start | bytes 1277960 | tf_op jit(solution)/shard_map/ppermute | solution.py:295
  107.3 10.5 %copy-start.3 = (bf16[832,512]{1,0:T(8,128)(2,1)}, bf16[832,512]{1,0:T(8,128)(2,1)S(1)}, u32[]{:S(2)}) copy-start(bf16[832,512]{1,0:T(8,128)(2,1)S(1)} %constant_dynamic-update-slice_fusion.4.x_ref) | copy-start | bytes 2555908
  107.3 16.4 %collective-permute-start.15 = (bf16[832,512]{1,0:T(8,128)(2,1)S(1)}, bf16[832,512]{1,0:T(8,128)(2,1)S(1)}, u32[]{:S(2)}, u32[]{:S(2)}) collective-permute-start(bf16[832,512]{1,0:T(8,128)(2,1)S(1)} %constant_dynamic-update-slice_fusion.4.x_ref), channel_id=1, source_target_pairs={{0,1},{1,0},{2,3},{3,2},{4,5},{5,4},{6,7},{7,6},{8,9},{9,8},{10,11... | collective-permute-start | bytes 2555912 | tf_op jit(solution)/shard_map/ppermute | solution.py:295
  109.1 8.7 %copy-start.2 = (bf16[832,512]{1,0:T(8,128)(2,1)}, bf16[832,512]{1,0:T(8,128)(2,1)S(1)}, u32[]{:S(2)}) copy-start(bf16[832,512]{1,0:T(8,128)(2,1)S(1)} %constant_dynamic-update-slice_fusion.z_ref) | copy-start | bytes 2555908
  109.1 14.6 %collective-permute-start.11 = (bf16[832,512]{1,0:T(8,128)(2,1)S(1)}, bf16[832,512]{1,0:T(8,128)(2,1)S(1)}, u32[]{:S(2)}, u32[]{:S(2)}) collective-permute-start(bf16[832,512]{1,0:T(8,128)(2,1)S(1)} %constant_dynamic-update-slice_fusion.z_ref), channel_id=1, source_target_pairs={{0,1},{1,0},{2,3},{3,2},{4,5},{5,4},{6,7},{7,6},{8,9},{9,8},{10,11... | collective-permute-start | bytes 2555912 | tf_op jit(solution)/shard_map/ppermute | solution.py:295
  (5 other events, 4.8 us)
where the time goes:
time: 132 us; the launch traced here: 131 us
  Pallas kernels  50.1 us (38%)
  waiting for transfers between devices  42.5 us (32%)
  starting transfers between devices  25.2 us (19%)
  local copies, waits for them, and re-layouts  8.94 us (7%)
  other arithmetic  4 us (3%)
    ppermute x16, waiting for transfers between devices, trade(): lax.ppermute(value, 'ga', [(i, i ^ 1 << bit) for i in range(members)])  37 us
    ppermute x16, starting transfers between devices, trade(): lax.ppermute(value, 'ga', [(i, i ^ 1 << bit) for i in range(members)])  17.8 us
    pallas_call x3, Pallas kernels, project(): pl.pallas_call(project_kernel, out_shape=jax.ShapeDtypeStruct((left.shape...  11.9 us
    pallas_call x1, Pallas kernels, prepare_ket(): pl.pallas_call(functools.partial(ket_kernel, atoms, size, block), grid=(2...  8.65 us
    all_to_all x1, starting transfers between devices, on_device(): lax.all_to_all(packed.reshape(groups, capacity, -1), 'ga', split_axis=0,...  7.41 us
    pallas_call x1, Pallas kernels, prepare_bra(): pl.pallas_call(functools.partial(bra_kernel, atoms, size), grid=(2,), in_...  7.16 us
    pallas_call x1, Pallas kernels, back_last(): pl.pallas_call(back_last_kernel, out_shape=jax.ShapeDtypeStruct((2, left....  6 us
    pallas_call x1, Pallas kernels, back_first(): pl.pallas_call(back_first_kernel, out_shape=jax.ShapeDtypeStruct((2, left...  5.88 us
  transfers between devices with their start and end apart: 17, of which 11 were waited for; matrix products, arithmetic and copies ran while one was open for 7% of the time, Pallas kernels for 24%

commit v1 on v0

v1 whole, which is shorter than its diff:
```python
import functools

import jax
import jax.numpy as jnp
import numpy as np
from jax import lax
from jax.experimental import pallas as pl
from jax.experimental.pallas import tpu as pltpu
from jax.sharding import PartitionSpec as P

F32, BF16 = jnp.float32, jnp.bfloat16
LANES = 128
SMEM = pl.BlockSpec(memory_space=pltpu.SMEM)


def stage_bits(count):
    first = list(range(count))
    second = list(first)
    if count > 2:
        second[1], second[2] = 2, 1
    return first, second


def block_order(bits):
    count = len(bits)
    return [
        sum(((place >> (count - 1 - i)) & 1) << bits[i] for i in range(count))
        for place in range(1 << count)
    ]


VMEM = pltpu.VMEM
WHOLE = pl.BlockSpec(memory_space=pltpu.VMEM)
ANY = pl.BlockSpec(memory_space=pl.ANY)
MIB = 1 << 20


def call(kernel, outs, args, flops, limit, after=()):
    def body(*refs):
        kernel(*refs[len(after) :])

    body.__name__ = kernel.__name__
    moved = sum(a.size * a.dtype.itemsize for a in args)
    return pl.pallas_call(
        body,
        out_shape=[VMEM(shape, kind) for shape, kind in outs],
        in_specs=[ANY] * len(after) + [WHOLE] * len(args),
        out_specs=[WHOLE] * len(outs),
        compiler_params=pltpu.CompilerParams(vmem_limit_bytes=limit * MIB),
        cost_estimate=pl.CostEstimate(flops=flops, bytes_accessed=moved, transcendentals=0),
    )(*after, *[pltpu.with_memory_space_constraint(a, VMEM) for a in args])


def pack_kernel(send_ref, psi_ref, out_ref):
    groups, capacity = send_ref.shape
    rows, slots, bands = psi_ref.shape[1], groups * capacity, psi_ref.shape[2]
    lane = lax.broadcasted_iota(jnp.int32, (capacity, slots), 1)
    inner = lax.broadcasted_iota(jnp.int32, (capacity, slots), 0)
    spread = jnp.dot(
        send_ref[...].astype(F32),
        (lane % capacity == inner).astype(F32),
        precision=lax.Precision.HIGHEST,
        preferred_element_type=F32,
    )
    lane = lax.broadcasted_iota(jnp.int32, (groups, slots), 1)
    outer = lax.broadcasted_iota(jnp.int32, (groups, slots), 0)
    flat = jnp.sum(jnp.where(lane // capacity == outer, spread, 0.0), axis=0, keepdims=True)
    row = lax.broadcasted_iota(jnp.int32, (rows, slots), 0)
    chosen = (row == flat.astype(jnp.int32)).astype(BF16)
    for part in range(2):
        picked = lax.dot_general(
            chosen, psi_ref[part], (((0,), (0,)), ((), ())), preferred_element_type=F32
        )
        out_ref[:, part * bands : (part + 1) * bands] = picked.astype(BF16)


def pack_rows(send, psi):
    count = send.shape[0] * send.shape[1]
    return pl.pallas_call(
        pack_kernel,
        out_shape=jax.ShapeDtypeStruct((count, 2 * psi.shape[2]), BF16),
        compiler_params=pltpu.CompilerParams(vmem_limit_bytes=12 * MIB),
        cost_estimate=pl.CostEstimate(
            flops=300_000_000, bytes_accessed=1_000_000, transcendentals=0
        ),
    )(send, psi)


def place_kernel(recv_ref, out_ref):
    chosen = lax.broadcasted_iota(jnp.int32, out_ref.shape, 0) == recv_ref[...]
    out_ref[...] = chosen.astype(F32).T.astype(BF16)


def place_matrix(recv, slots):
    return call(place_kernel, [((recv.shape[1], slots), BF16)], [recv], 1_000_000_000, 8)[0]


def widen_rows(source, part, wide):
    rows, step = source.shape[1], 96
    while rows % step:
        step -= 8

    def body(index, carry):
        start = pl.multiple_of(index * step, 8)
        for l in range(wide.shape[0]):
            lanes = slice(LANES * l, LANES * (l + 1))
            wide[l, pl.ds(start, step), :] = source[part, pl.ds(start, step), lanes].astype(F32)
        return carry

    lax.fori_loop(0, rows // step, body, 0)


def walk_atoms(wide, tables, vectors, place, atoms, size, store):
    home, order, displaced, mode = tables
    base = (home[0] ^ order[place]) * atoms
    for i in range(atoms):
        start = displaced[base + i] * size
        amount = [mode[x, base + i] for x in range(3)]
        for l in range(wide.shape[0]):
            lanes = slice(LANES * l, LANES * (l + 1))
            picked = wide[l, pl.ds(start, size), :]
            weight = (
                amount[0] * vectors[0:1, lanes]
                + amount[1] * vectors[1:2, lanes]
                + amount[2] * vectors[2:3, lanes]
            )
            store(i, l, picked, weight)


def bra_kernel(atoms, size, tables, source, vectors, plain, scaled, wide, slabs, finished):
    half, block = plain[0].shape[1:3]
    swap = tables[1]
    tables = (tables[0], *tables[2:])
    slab, slab_scaled = slabs
    if block != atoms * size:
        slab[...] = jnp.zeros_like(slab)
        slab_scaled[...] = jnp.zeros_like(slab_scaled)

    def store(i, l, picked, weight):
        slab[l, size * i : size * (i + 1), :] = picked
        slab_scaled[l, size * i : size * (i + 1), :] = picked * weight

    for part in range(2):
        widen_rows(source, part, wide)
        for h in range(2):

            def body(index, carry):
                place = h * half + index
                walk_atoms(wide, tables, vectors, place, atoms, size, store)
                other = swap[place] - h * half
                for l in range(wide.shape[0]):
                    lanes = slice(LANES * l, LANES * (l + 1))
                    plain[h][part, index, :, lanes] = slab[l].astype(BF16)
                    scaled[h][part, other, :, lanes] = slab_scaled[l].astype(BF16)
                return carry

            lax.fori_loop(0, half, body, 0)
        finished(part)


def ket_kernel(atoms, size, block, tables, source, vectors, turned, wide, slab):
    half = slab.shape[1] // (2 * block)
    swap = tables[1]
    tables = (tables[0], *tables[2:])
    if block != atoms * size:
        slab[...] = jnp.zeros_like(slab)
    for part in range(2):
        widen_rows(source, part, wide)
        for h in range(2):

            def body(index, carry):
                place = h * half + index
                plain_row = pl.multiple_of((swap[place] - h * half) * block, 8)
                scaled_row = pl.multiple_of((half + index) * block, 8)

                def store(i, l, picked, weight):
                    slab[l, pl.ds(plain_row + size * i, size), :] = picked
                    slab[l, pl.ds(scaled_row + size * i, size), :] = -(picked * weight)

                walk_atoms(wide, tables, vectors, place, atoms, size, store)
                return carry

            lax.fori_loop(0, half, body, 0)
            for j in range(slab.shape[1] // LANES):
                columns = slice(LANES * j, LANES * (j + 1))
                for l in range(wide.shape[0]):
                    lanes = slice(LANES * l, LANES * (l + 1))
                    turned[h][part, lanes, columns] = slab[l, columns, :].T.astype(BF16)


def prepare_bra(tables, beta, vectors, atoms, size, block, after):
    half = tables[1].shape[0] // 2
    rows, width = beta.shape[1:]
    tiles = width // LANES
    skip = len(after)
    shape = (2, half, block, width)

    def body(*refs):
        home, swap, order, displaced, mode, source, vectors_ref = refs[skip : skip + 7]
        ready, outs = refs[skip + 7], refs[skip + 8 : skip + 11]
        staged, sent, scratch = refs[skip + 11 : skip + 14], refs[skip + 14], refs[skip + 15 :]
        copies = [
            [
                pltpu.make_async_copy(staged[n].at[part], outs[n].at[part], sent.at[n, part])
                for n in range(3)
            ]
            for part in range(2)
        ]

        def finished(part):
            for copy in copies[part]:
                copy.start()

        bra_kernel(
            atoms, size, (home, swap, order, displaced, mode), source, vectors_ref,
            (staged[0], ready), (staged[1], staged[2]), scratch[0], scratch[1:3], finished,
        )
        for group in copies:
            for copy in group:
                copy.wait()

    ready, *rest = pl.pallas_call(
        body,
        in_specs=[ANY] * skip + [SMEM] * 5 + [WHOLE, WHOLE],
        out_specs=[WHOLE] + [pl.BlockSpec(memory_space=pltpu.HBM)] * 3,
        out_shape=[VMEM(shape, BF16)] + [pltpu.HBM(shape, BF16)] * 3,
        scratch_shapes=[VMEM(shape, BF16)] * 3
        + [
            pltpu.SemaphoreType.DMA((3, 2)),
            VMEM((tiles, rows, LANES), F32),
            VMEM((tiles, block, LANES), F32),
            VMEM((tiles, block, LANES), F32),
        ],
        compiler_params=pltpu.CompilerParams(vmem_limit_bytes=14 * MIB),
        cost_estimate=pl.CostEstimate(
            flops=8_000_000_000, bytes_accessed=12_000_000, transcendentals=0
        ),
    )(*after, *tables, pltpu.with_memory_space_constraint(beta, VMEM), vectors)
    return rest[0], ready, rest[1], rest[2]


def prepare_ket(tables, beta, vectors, atoms, size, block, after):
    half = tables[1].shape[0] // 2
    rows, width = beta.shape[1:]
    tiles, depth = width // LANES, 2 * half * block
    skip = len(after)

    def body(*refs):
        home, swap, order, displaced, mode, source, vectors_ref = refs[skip : skip + 7]
        outs, token, scratch = refs[skip + 7 : skip + 9], refs[skip + 9], refs[skip + 10 :]
        ket_kernel(
            atoms, size, block, (home, swap, order, displaced, mode), source, vectors_ref,
            outs, *scratch,
        )
        token[...] = jnp.zeros_like(token)

    return pl.pallas_call(
        body,
        in_specs=[ANY] * skip + [SMEM] * 5 + [WHOLE, WHOLE],
        out_specs=[WHOLE] * 3,
        out_shape=[VMEM((2, width, depth), BF16)] * 2 + [VMEM((8, LANES), F32)],
        scratch_shapes=[
            VMEM((tiles, rows, LANES), F32),
            VMEM((tiles, depth, LANES), F32),
        ],
        compiler_params=pltpu.CompilerParams(vmem_limit_bytes=14 * MIB),
        cost_estimate=pl.CostEstimate(
            flops=8_000_000_000, bytes_accessed=12_000_000, transcendentals=0
        ),
    )(*after, *tables, pltpu.with_memory_space_constraint(beta, VMEM), vectors)


def project_kernel(waves_ref, left_ref, out_ref):
    total = jnp.dot(left_ref[0], waves_ref[0], preferred_element_type=F32)
    total += jnp.dot(left_ref[1], waves_ref[1], preferred_element_type=F32)
    out_ref[...] = total.astype(out_ref.dtype)


def wave_kernel(arrived_ref, place_ref, left_ref, waves_ref, out_ref):
    bands = arrived_ref.shape[1] // 2
    rows = jnp.dot(place_ref[...], arrived_ref[...], preferred_element_type=F32).astype(BF16)
    waves_ref[0] = rows
    waves_ref[1, :, :bands] = rows[:, bands:]
    waves_ref[1, :, bands:] = -rows[:, :bands]
    project_kernel(waves_ref, left_ref, out_ref)


def first_project(arrived, place, left):
    width = arrived.shape[1]
    outs = [((2, place.shape[0], width), BF16), ((left.shape[1], width), BF16)]
    return call(wave_kernel, outs, [arrived, place, left], 1_200_000_000, 14)


def project(waves, left, kind, after=()):
    outs = [((left.shape[1], waves.shape[2]), kind)]
    return call(project_kernel, outs, [waves, left], 900_000_000, 14, after)[0]


def fold_kernel(kept_ref, came_ref, next_ref, away_ref):
    rows = next_ref.shape[0]
    next_ref[...] = kept_ref[:rows] + came_ref[:rows].astype(F32)
    away_ref[...] = (kept_ref[rows:] + came_ref[rows:].astype(F32)).astype(BF16)


def fold(kept, came, after=()):
    rows, width = kept.shape[0] // 2, kept.shape[1]
    outs = [((rows, width), F32), ((rows, width), BF16)]
    return call(fold_kernel, outs, [kept, came], 1_000_000, 4, after)


def couple_kernel(matrix_ref, *refs):
    for kept, came, out in zip(refs[0:2], refs[2:4], refs[4:6]):
        out[...] = jnp.dot(
            matrix_ref[...],
            kept[...] + came[...].astype(F32),
            precision=lax.Precision.HIGHEST,
            preferred_element_type=F32,
        ).astype(BF16)


def couple(matrix, kept, came):
    outs = [(kept[0].shape, BF16)] * 2
    return call(couple_kernel, outs, [matrix, *kept, *came], 200_000_000, 6)


def join_kernel(own_ref, came_ref, out_ref):
    rows = own_ref.shape[0]
    out_ref[:rows] = own_ref[...]
    out_ref[rows:] = came_ref[...]


def join(own, came):
    outs = [((2 * own.shape[0], own.shape[1]), BF16)]
    return call(join_kernel, outs, [own, came], 1_000_000, 4)[0]


def back_kernel(low, high, start, left_ref, *refs):
    out_ref = refs[-1]
    right = jnp.concatenate([ref[...] for ref in refs[: len(refs) - 1 - start]], axis=0)
    right = right[: high - low]
    total = []
    for part in range(2):
        product = jnp.dot(left_ref[part, :, low:high], right, preferred_element_type=F32)
        total.append(refs[-2][part] + product if start else product)
    if out_ref.dtype == F32:
        out_ref[0], out_ref[1] = total
    else:
        bands = out_ref.shape[2]
        real, imag = total
        out_ref[0] = (-(real[:, bands:] + imag[:, :bands])).astype(BF16)
        out_ref[1] = (real[:, :bands] - imag[:, bands:]).astype(BF16)


def back_partial(left, low, high, rights, start=()):
    kernel = functools.partial(back_kernel, low, high, len(start))
    kernel.__name__ = "back_kernel"
    outs = [((2, left.shape[1], rights[0].shape[1]), F32)]
    flops = 4 * left.shape[1] * (high - low) * rights[0].shape[1]
    return call(kernel, outs, [left, *rights, *start], flops, 20)[0]


def back_last(left, high, rights, start):
    args = [left, *rights, start]
    return pl.pallas_call(
        functools.partial(back_kernel, 0, high, 1),
        in_specs=[WHOLE] * len(args),
        out_specs=WHOLE,
        out_shape=jax.ShapeDtypeStruct((2, left.shape[1], rights[0].shape[1] // 2), BF16),
        compiler_params=pltpu.CompilerParams(vmem_limit_bytes=20 * MIB),
        cost_estimate=pl.CostEstimate(
            flops=2_000_000_000, bytes_accessed=6_000_000, transcendentals=0
        ),
    )(*[pltpu.with_memory_space_constraint(a, VMEM) for a in args])


def trade(value, bit):
    members = lax.axis_size("ga")
    return lax.ppermute(value, "ga", [(i, i ^ (1 << bit)) for i in range(members)])


def on_device(psi_k, beta_k, beta_kq, g_k, g_kq, send_index, recv_index, dmat, displaced, mode):
    groups = lax.axis_size("ga")
    count = groups.bit_length() - 1
    capacity = send_index.shape[2]
    slots = groups * capacity
    size = dmat.shape[1]
    atoms = displaced.shape[0] // groups
    block = -(-atoms * size // 8) * 8
    if block * groups % LANES:
        block = -(-block // 16) * 16
    me = lax.axis_index("ga").astype(jnp.int32)
    streams = stage_bits(count)
    orders = [block_order(bits) for bits in streams]
    swap = np.array([orders[1].index(k) for k in orders[0]], np.int32)
    tables = (
        me.reshape(1),
        jnp.asarray(swap),
        jnp.asarray(np.array(orders[0], np.int32)),
        displaced,
        mode,
    )

    packed = pack_rows(send_index[0], psi_k)
    arrived = lax.all_to_all(
        packed.reshape(groups, capacity, -1), "ga", split_axis=0, concat_axis=0, tiled=True
    ).reshape(slots, -1)

    own = lax.dynamic_slice_in_dim(displaced, me * atoms, atoms)
    coupling = jnp.take(dmat, own, axis=0)
    matrix = (jnp.eye(atoms, dtype=F32)[:, None, :, None] * coupling[:, :, None, :]).reshape(
        atoms * size, atoms * size
    )
    spare = block - atoms * size
    matrix = jnp.pad(matrix, ((0, spare), (0, spare)))
    place = place_matrix(recv_index.reshape(1, -1), slots)
    lefts = prepare_bra(
        tables, jnp.swapaxes(beta_k, 1, 2), g_k, atoms, size, block, (matrix[:1, :1],)
    )
    lefts = [left.reshape(2, -1, left.shape[3]) for left in lefts]

    waves, away_first = first_project(arrived, place, lefts[1])
    came_first = trade(away_first, streams[0][0])
    away_second = project(waves, lefts[3], BF16)
    came_second = trade(away_second, streams[1][0])
    kept = [project(waves, lefts[0], F32), project(waves, lefts[2], F32)]
    came = [came_first, came_second]
    token = ()
    for stage in range(1, count):
        away = [None, None]
        for s in range(2):
            behind = () if s == 0 else (away[0][:8, :LANES],)
            kept[s], away[s] = fold(kept[s], came[s], (*token, *behind))
        came = [trade(away[s], streams[s][stage]) for s in range(2)]
        if stage == 1:
            *turned, token = prepare_ket(
                tables, jnp.swapaxes(beta_kq, 1, 2), g_kq, atoms, size, block,
                (away[0][:8, :LANES], away[1][:8, :LANES]),
            )
            token = (token,)
        else:
            token = ()

    gathered = list(couple(matrix, kept, came))
    for stage in range(count - 1, 0, -1):
        came = [trade(gathered[s], streams[s][stage]) for s in range(2)]
        gathered = [join(gathered[s], came[s]) for s in range(2)]
    came = [trade(gathered[s], streams[s][0]) for s in range(2)]
    rows = gathered[0].shape[0]
    start = back_partial(turned[0], 0, 2 * rows, [gathered[1], gathered[0]])
    cut = -(-rows // LANES) * LANES
    start = back_partial(turned[1], cut, 2 * rows, [came[0][cut - rows :]], [start])
    return back_last(turned[1], cut, [came[1], came[0][: max(cut - rows, 8)]], start)


def solution(mesh):
    in_specs = (
        P(None, "ga", None),
        P(None, "ga", None),
        P(None, "ga", None),
        P(None, "ga"),
        P(None, "ga"),
        P("ga", None, None),
        P("ga"),
        P(),
        P("pert"),
        P(None, "pert"),
    )
    out_specs = P("pert", "ga", None)
    return jax.shard_map(
        on_device, mesh=mesh, in_specs=in_specs, out_specs=out_specs, check_vma=False
    )
```

time: 132 us -> 95.4 us (0.72)
  Pallas kernels: 50.1 us -> 24.9 us
  other arithmetic: 4 us -> 0.27 us
  waiting for transfers between devices: 42.5 us -> 38.9 us
  starting transfers between devices: 25.2 us -> 23.2 us
  local copies, waits for them, and re-layouts: 8.94 us -> 7.34 us
    pallas_call x10 -> x23, Pallas kernels: 47.8 us -> 23.4 us  [the longest x20 8.99 us: call(): pl.pallas_call(body, out_shape=[VMEM(shape, kind) for shape, kind in outs...]
    all_to_all x1, waiting for transfers between devices: 5.42 us -> 2.21 us  [on_device(): lax.all_to_all(packed.reshape(groups, capacity, -1), 'ga', split_axis=0,...]
    concatenate x4 -> x0, other arithmetic: 2.78 us -> none  [on_device(): jnp.concatenate([gathered[s], came[s]], axis=0)]
    ppermute x16, starting transfers between devices: 17.8 us -> 15.8 us  [trade(): lax.ppermute(value, 'ga', [(i, i ^ 1 << bit) for i in range(members)])]
    unnamed x30 -> x33, local copies, waits for them, and re-layouts: 4.59 us -> 5.97 us
    reshape x1 -> x0, local copies, waits for them, and re-layouts: 1.37 us -> none  [on_device(): packed = pack_rows(send_index.reshape(1, slots), psi_k)]
  transfers between devices with their start and end apart: 17 -> 17, of which waited for: 11 -> 12; matrix products, arithmetic and copies ran while one was open for 7% -> 3% of each run, Pallas kernels for 24% -> 20%
where the time goes in v1:
time: 95.4 us; the launch traced here: 95 us
  waiting for transfers between devices  38.9 us (41%)
  Pallas kernels  24.9 us (26%)
  starting transfers between devices  23.2 us (24%)
  local copies, waits for them, and re-layouts  7.34 us (8%)
    ppermute x16, waiting for transfers between devices, trade(): lax.ppermute(value, 'ga', [(i, i ^ 1 << bit) for i in range(members)])  36.7 us
    ppermute x16, starting transfers between devices, trade(): lax.ppermute(value, 'ga', [(i, i ^ 1 << bit) for i in range(members)])  15.8 us
    pallas_call x20, Pallas kernels, call(): pl.pallas_call(body, out_shape=[VMEM(shape, kind) for shape, kind in outs...  8.99 us
    all_to_all x1, starting transfers between devices, on_device(): lax.all_to_all(packed.reshape(groups, capacity, -1), 'ga', split_axis=0,...  7.41 us
    pallas_call x1, Pallas kernels, prepare_bra(): pl.pallas_call(body, in_specs=[ANY] * skip + [SMEM] * 5 + [WHOLE, WHOLE],...  6.39 us
    pallas_call x1, Pallas kernels, prepare_ket(): pl.pallas_call(body, in_specs=[ANY] * skip + [SMEM] * 5 + [WHOLE, WHOLE],...  6.02 us
    unnamed x33, local copies, waits for them, and re-layouts  5.97 us
    all_to_all x1, waiting for transfers between devices, on_device(): lax.all_to_all(packed.reshape(groups, capacity, -1), 'ga', split_axis=0,...  2.21 us
  transfers between devices with their start and end apart: 17, of which 12 were waited for; matrix products, arithmetic and copies ran while one was open for 3% of the time, Pallas kernels for 20%

profile of v1, /device:TPU:0, one launch (start us, length us, event | category | flops | bytes accessed | tf_op | source)
XLA Modules:
  0.0 95.0 jit_solution(913725212385224993)
XLA Ops:
  1.8 1.4 %shard_map.118 = bf16[512,512]{1,0:T(8,128)(2,1)} custom-call(s32[16,32]{1,0:T(8,128)S(1)} %bitcast.21, bf16[2,512,256]{2,1,0:T(8,128)(2,1)S(1)} %copy-done.5), custom_call_target="tpu_custom_call" | custom-call | flops 300000000 | bytes 1000000 | tf_op jit(solution)/shard_map/pallas_call | solution.py:79
  3.2 7.4 %all-to-all-start = ((bf16[16,32,512]{2,1,0:T(8,128)(2,1)}), bf16[16,32,512]{2,1,0:T(8,128)(2,1)S(1)}, u32[]{:S(2)}, u32[]{:S(2)}) async-start(bf16[16,32,512]{2,1,0:T(8,128)(2,1)} %bitcast.1), calls=%async_computation | async-start | bytes 1048576 | tf_op jit(solution)/shard_map/all_to_all | solution.py:404
  13.8 2.4 %copy-done.4 = bf16[2,512,2496]{1,2,0:T(8,128)(2,1)S(1)} copy-done((bf16[2,512,2496]{1,2,0:T(8,128)(2,1)S(1)}, bf16[2,512,2496]{1,2,0:T(8,128)(2,1)}, u32[]{:S(2)}) %copy-start.4) | copy-done | bytes 5111832
  16.3 6.4 %shard_map.120 = (bf16[2,8,104,512]{3,2,1,0:T(8,128)(2,1)S(1)}, bf16[2,8,104,512]{3,2,1,0:T(8,128)(2,1)}, bf16[2,8,104,512]{3,2,1,0:T(8,128)(2,1)}, bf16[2,8,104,512]{3,2,1,0:T(8,128)(2,1)}) custom-call(f32[1,1]{1,0:T(1,128)} %slice.31.refs_0_, s32[1]{0:T(128)} %bitcast.4.refs_1_.refs_2_, s32[16]{0:T(128)S(1)} %copy-done.12, s32[16]{0:T(128)S(1)} %copy-done.11, ...), custom_call_target="tpu_custom_call" | custom-call | flops 8000000000 | bytes 12000000 | tf_op jit(solution)/shard_map/pallas_call | solution.py:222
  22.7 2.2 %all-to-all-done = bf16[16,32,512]{2,1,0:T(8,128)(2,1)S(1)} async-done(((bf16[16,32,512]{2,1,0:T(8,128)(2,1)}), bf16[16,32,512]{2,1,0:T(8,128)(2,1)S(1)}, u32[]{:S(2)}, u32[]{:S(2)}) %all-to-all-start) | async-done | bytes 524320 | tf_op jit(solution)/shard_map/all_to_all | solution.py:404
  24.9 1.4 %shard_map.121 = (bf16[2,512,512]{2,1,0:T(8,128)(2,1)S(1)}, bf16[832,512]{1,0:T(8,128)(2,1)S(1)}) custom-call(bf16[512,512]{1,0:T(8,128)(2,1)S(1)} %bitcast.16, bf16[512,512]{1,0:T(8,128)(2,1)S(1)} %shard_map.119.refs_1_, bf16[2,832,512]{2,1,0:T(8,128)(2,1)S(1)} %bitcast.23), custom_call_target="tpu_custom_call" | custom-call | flops 1200000000 | bytes 2752512 | tf_op jit(solution)/shard_map/pallas_call | solution.py:44
  30.7 1.3 %collective-permute-start.2 = (bf16[416,512]{1,0:T(8,128)(2,1)S(1)}, bf16[416,512]{1,0:T(8,128)(2,1)S(1)}, u32[]{:S(2)}, u32[]{:S(2)}) collective-permute-start(bf16[416,512]{1,0:T(8,128)(2,1)S(1)} %get-tuple-element.32), channel_id=1, source_target_pairs={{0,2},{1,3},{2,0},{3,1},{4,6},{5,7},{6,4},{7,5},{8,10},{9,11},{10,... | collective-permute-start | bytes 1277960 | tf_op jit(solution)/shard_map/ppermute | solution.py:378
  32.1 1.5 %collective-permute-start.4 = (bf16[416,512]{1,0:T(8,128)(2,1)S(1)}, bf16[416,512]{1,0:T(8,128)(2,1)S(1)}, u32[]{:S(2)}, u32[]{:S(2)}) collective-permute-start(bf16[416,512]{1,0:T(8,128)(2,1)S(1)} %get-tuple-element.35), channel_id=1, source_target_pairs={{0,4},{1,5},{2,6},{3,7},{4,0},{5,1},{6,2},{7,3},{8,12},{9,13},{10,... | collective-permute-start | bytes 1277960 | tf_op jit(solution)/shard_map/ppermute | solution.py:378
  33.6 6.0 %shard_map.127 = (bf16[2,512,1664]{2,1,0:T(8,128)(2,1)S(1)}, bf16[2,512,1664]{2,1,0:T(8,128)(2,1)S(1)}, f32[8,128]{1,0:T(8,128)S(1)}) custom-call(bf16[8,128]{1,0:T(8,128)(2,1)S(1)} %slice.23.refs_0_, bf16[8,128]{1,0:T(8,128)(2,1)S(1)} %slice.24.refs_1_, s32[1]{0:T(128)} %bitcast.4.refs_1_.refs_2_, s32[16]{0:T(128)S(1)} %copy-done.12, s32[16]{0:T(128)S(1)} %copy-done.11, ...), custom_call_target="tpu_custom_call" | custom-call | flops 8000000000 | bytes 12000000 | tf_op jit(solution)/shard_map/pallas_call | solution.py:257
  39.6 3.2 %collective-permute-done.2.refs_2_ = bf16[416,512]{1,0:T(8,128)(2,1)S(1)} collective-permute-done((bf16[416,512]{1,0:T(8,128)(2,1)S(1)}, bf16[416,512]{1,0:T(8,128)(2,1)S(1)}, u32[]{:S(2)}, u32[]{:S(2)}) %collective-permute-start.2) | collective-permute-done | bytes 426016 | tf_op jit(solution)/shard_map/ppermute | solution.py:378
  42.9 1.6 %collective-permute-start.3 = (bf16[208,512]{1,0:T(8,128)(2,1)S(1)}, bf16[208,512]{1,0:T(8,128)(2,1)S(1)}, u32[]{:S(2)}, u32[]{:S(2)}) collective-permute-start(bf16[208,512]{1,0:T(8,128)(2,1)S(1)} %get-tuple-element.40), channel_id=1, source_target_pairs={{0,4},{1,5},{2,6},{3,7},{4,0},{5,1},{6,2},{7,3},{8,12},{9,13},{10,... | collective-permute-start | bytes 638984 | tf_op jit(solution)/shard_map/ppermute | solution.py:378
  45.6 4.0 %collective-permute-done.3.refs_1_ = bf16[208,512]{1,0:T(8,128)(2,1)S(1)} collective-permute-done((bf16[208,512]{1,0:T(8,128)(2,1)S(1)}, bf16[208,512]{1,0:T(8,128)(2,1)S(1)}, u32[]{:S(2)}, u32[]{:S(2)}) %collective-permute-start.3) | collective-permute-done | bytes 213024 | tf_op jit(solution)/shard_map/ppermute | solution.py:378
  49.6 1.2 %collective-permute-done.5.refs_2_ = bf16[208,512]{1,0:T(8,128)(2,1)S(1)} collective-permute-done((bf16[208,512]{1,0:T(8,128)(2,1)S(1)}, bf16[208,512]{1,0:T(8,128)(2,1)S(1)}, u32[]{:S(2)}, u32[]{:S(2)}) %collective-permute-start.5) | collective-permute-done | bytes 213024 | tf_op jit(solution)/shard_map/ppermute | solution.py:378
  50.9 1.5 %collective-permute-start.7 = (bf16[104,512]{1,0:T(8,128)(2,1)S(1)}, bf16[104,512]{1,0:T(8,128)(2,1)S(1)}, u32[]{:S(2)}, u32[]{:S(2)}) collective-permute-start(bf16[104,512]{1,0:T(8,128)(2,1)S(1)} %get-tuple-element.47), channel_id=1, source_target_pairs={{0,8},{1,9},{2,10},{3,11},{4,12},{5,13},{6,14},{7,15},{8,0},{9,1},... | collective-permute-start | bytes 319496 | tf_op jit(solution)/shard_map/ppermute | solution.py:378
  52.4 1.5 %collective-permute-start.6 = (bf16[104,512]{1,0:T(8,128)(2,1)S(1)}, bf16[104,512]{1,0:T(8,128)(2,1)S(1)}, u32[]{:S(2)}, u32[]{:S(2)}) collective-permute-start(bf16[104,512]{1,0:T(8,128)(2,1)S(1)} %get-tuple-element.42), channel_id=1, source_target_pairs={{0,8},{1,9},{2,10},{3,11},{4,12},{5,13},{6,14},{7,15},{8,0},{9,1},... | collective-permute-start | bytes 319496 | tf_op jit(solution)/shard_map/ppermute | solution.py:378
  53.9 6.7 %collective-permute-done.7.refs_4_ = bf16[104,512]{1,0:T(8,128)(2,1)S(1)} collective-permute-done((bf16[104,512]{1,0:T(8,128)(2,1)S(1)}, bf16[104,512]{1,0:T(8,128)(2,1)S(1)}, u32[]{:S(2)}, u32[]{:S(2)}) %collective-permute-start.7) | collective-permute-done | bytes 106528 | tf_op jit(solution)/shard_map/ppermute | solution.py:378
  62.4 2.9 %collective-permute-start.8 = (bf16[104,512]{1,0:T(8,128)(2,1)S(1)}, bf16[104,512]{1,0:T(8,128)(2,1)S(1)}, u32[]{:S(2)}, u32[]{:S(2)}) collective-permute-start(bf16[104,512]{1,0:T(8,128)(2,1)S(1)} %get-tuple-element.48.refs_0_), channel_id=1, source_target_pairs={{0,8},{1,9},{2,10},{3,11},{4,12},{5,13},{6,14},{7,15},{8,0},{9,1},... | collective-permute-start | bytes 319496 | tf_op jit(solution)/shard_map/ppermute | solution.py:378
  65.3 7.4 %collective-permute-done.12.refs_1_ = bf16[104,512]{1,0:T(8,128)(2,1)S(1)} collective-permute-done((bf16[104,512]{1,0:T(8,128)(2,1)S(1)}, bf16[104,512]{1,0:T(8,128)(2,1)S(1)}, u32[]{:S(2)}, u32[]{:S(2)}) %collective-permute-start.12) | collective-permute-done | bytes 106528 | tf_op jit(solution)/shard_map/ppermute | solution.py:378
  74.9 3.8 %collective-permute-done.13.refs_1_ = bf16[208,512]{1,0:T(8,128)(2,1)S(1)} collective-permute-done((bf16[208,512]{1,0:T(8,128)(2,1)S(1)}, bf16[208,512]{1,0:T(8,128)(2,1)S(1)}, u32[]{:S(2)}, u32[]{:S(2)}) %collective-permute-start.13) | collective-permute-done | bytes 213024 | tf_op jit(solution)/shard_map/ppermute | solution.py:378
  79.4 1.8 %collective-permute-done.9.refs_1_ = bf16[208,512]{1,0:T(8,128)(2,1)S(1)} collective-permute-done((bf16[208,512]{1,0:T(8,128)(2,1)S(1)}, bf16[208,512]{1,0:T(8,128)(2,1)S(1)}, u32[]{:S(2)}, u32[]{:S(2)}) %collective-permute-start.9) | collective-permute-done | bytes 213024 | tf_op jit(solution)/shard_map/ppermute | solution.py:378
  81.3 1.9 %collective-permute-start.10 = (bf16[416,512]{1,0:T(8,128)(2,1)S(1)}, bf16[416,512]{1,0:T(8,128)(2,1)S(1)}, u32[]{:S(2)}, u32[]{:S(2)}) collective-permute-start(bf16[416,512]{1,0:T(8,128)(2,1)S(1)} %shard_map.134.refs_0_), channel_id=1, source_target_pairs={{0,4},{1,5},{2,6},{3,7},{4,0},{5,1},{6,2},{7,3},{8,12},{9,13},{10,... | collective-permute-start | bytes 1277960 | tf_op jit(solution)/shard_map/ppermute | solution.py:378
  83.1 5.9 %collective-permute-done.14.refs_1_ = bf16[416,512]{1,0:T(8,128)(2,1)S(1)} collective-permute-done((bf16[416,512]{1,0:T(8,128)(2,1)S(1)}, bf16[416,512]{1,0:T(8,128)(2,1)S(1)}, u32[]{:S(2)}, u32[]{:S(2)}) %collective-permute-start.14) | collective-permute-done | bytes 426016 | tf_op jit(solution)/shard_map/ppermute | solution.py:378
  89.8 2.1 %shard_map.139.refs_2_ = f32[2,512,512]{2,1,0:T(8,128)S(1)} custom-call(bf16[2,512,1664]{2,1,0:T(8,128)(2,1)S(1)} %get-tuple-element.50.refs_0_, bf16[832,512]{1,0:T(8,128)(2,1)S(1)} %shard_map.135.refs_1_, bf16[832,512]{1,0:T(8,128)(2,1)S(1)} %shard_map.138.refs_2_), custom_call_target="tpu_custom_call" | custom-call | flops 1744830464 | bytes 5111808 | tf_op jit(solution)/shard_map/pallas_call | solution.py:44
  92.9 2.0 %shard_map.141 = bf16[2,512,256]{2,1,0:T(8,128)(2,1)} custom-call(bf16[2,512,1664]{2,1,0:T(8,128)(2,1)S(1)} %get-tuple-element.36.refs_0_.left_ref, bf16[832,512]{1,0:T(8,128)(2,1)S(1)} %collective-permute-done.11.refs_0_, bf16[64,512]{1,0:T(8,128)(2,1)S(1)} %slice.32.refs_1_, f32[2,512,512]{2,1,0:T(8,128)S(1)} %shard_map.140.refs_2_), custom_call_target="tpu_custom_call" | custom-call | flops 2000000000 | bytes 6000000 | tf_op jit(solution)/shard_map/pallas_call | solution.py:364
  (82 shorter events, 17.0 us)
Async XLA Ops:
  0.0 10.6 %copy-start.3 = (s32[128]{0:T(128)S(1)}, s32[128]{0:T(128)}, u32[]{:S(2)}) copy-start(s32[128]{0:T(128)} %refs_5_.3) | copy-start | bytes 1540
  1.8 9.0 %copy-start.13 = (f32[192,13,13]{0,2,1:T(8,128)S(1)}, f32[192,13,13]{0,2,1:T(8,128)}, u32[]{:S(2)}) copy-start(f32[192,13,13]{0,2,1:T(8,128)} %param.19) | copy-start | bytes 389380
  3.2 21.7 %all-to-all-start = ((bf16[16,32,512]{2,1,0:T(8,128)(2,1)}), bf16[16,32,512]{2,1,0:T(8,128)(2,1)S(1)}, u32[]{:S(2)}, u32[]{:S(2)}) async-start(bf16[16,32,512]{2,1,0:T(8,128)(2,1)} %bitcast.1), calls=%async_computation | async-start | bytes 1048576 | tf_op jit(solution)/shard_map/all_to_all | solution.py:404
  10.6 2.5 %copy-start.9 = (s32[512]{0:T(512)S(1)}, s32[512]{0:T(512)}, u32[]{:S(2)}) copy-start(s32[512]{0:T(512)} %param.18) | copy-start | bytes 6148
  13.8 2.5 %copy-start.4 = (bf16[2,512,2496]{1,2,0:T(8,128)(2,1)S(1)}, bf16[2,512,2496]{1,2,0:T(8,128)(2,1)}, u32[]{:S(2)}) copy-start(bf16[2,512,2496]{1,2,0:T(8,128)(2,1)} %param.13) | copy-start | bytes 15335428
  26.3 4.2 %collective-permute-start = (bf16[832,512]{1,0:T(8,128)(2,1)S(1)}, bf16[832,512]{1,0:T(8,128)(2,1)S(1)}, u32[]{:S(2)}, u32[]{:S(2)}) collective-permute-start(bf16[832,512]{1,0:T(8,128)(2,1)S(1)} %get-tuple-element.31), channel_id=1, source_target_pairs={{0,1},{1,0},{2,3},{3,2},{4,5},{5,4},{6,7},{7,6},{8,9},{9,8},{10,11... | collective-permute-start | bytes 2555912 | tf_op jit(solution)/shard_map/ppermute | solution.py:378
  27.5 4.4 %collective-permute-start.1 = (bf16[832,512]{1,0:T(8,128)(2,1)S(1)}, bf16[832,512]{1,0:T(8,128)(2,1)S(1)}, u32[]{:S(2)}, u32[]{:S(2)}) collective-permute-start(bf16[832,512]{1,0:T(8,128)(2,1)S(1)} %shard_map.125), channel_id=1, source_target_pairs={{0,1},{1,0},{2,3},{3,2},{4,5},{5,4},{6,7},{7,6},{8,9},{9,8},{10,11... | collective-permute-start | bytes 2555912 | tf_op jit(solution)/shard_map/ppermute | solution.py:378
  28.0 5.6 %slice-start = ((s8[5111808]{0:T(1024)(128)(4,1)}), s8[4194304]{0:T(1024)(128)(4,1)S(1)}, s32[]{:S(2)}) async-start(s8[5111808]{0:T(1024)(128)(4,1)} %bitcast.18), calls=%async_computation.1 | async-start | bytes 8388608
  29.4 4.2 %slice-start.1 = ((s8[5111808]{0:T(1024)(128)(4,1)}), s8[917504]{0:T(1024)(128)(4,1)S(1)}, s32[]{:S(2)}) async-start(s8[5111808]{0:T(1024)(128)(4,1)} %bitcast.18), calls=%async_computation.2 | async-start | bytes 1835008
  30.6 3.0 %copy-start.8 = (f32[3,512]{1,0:T(4,128)S(1)}, f32[3,512]{1,0:T(4,128)}, u32[]{:S(2)}) copy-start(f32[3,512]{1,0:T(4,128)} %refs_8_.1) | copy-start | bytes 18436
  30.7 12.1 %collective-permute-start.2 = (bf16[416,512]{1,0:T(8,128)(2,1)S(1)}, bf16[416,512]{1,0:T(8,128)(2,1)S(1)}, u32[]{:S(2)}, u32[]{:S(2)}) collective-permute-start(bf16[416,512]{1,0:T(8,128)(2,1)S(1)} %get-tuple-element.32), channel_id=1, source_target_pairs={{0,2},{1,3},{2,0},{3,1},{4,6},{5,7},{6,4},{7,5},{8,10},{9,11},{10,... | collective-permute-start | bytes 1277960 | tf_op jit(solution)/shard_map/ppermute | solution.py:378
  32.1 12.4 %collective-permute-start.4 = (bf16[416,512]{1,0:T(8,128)(2,1)S(1)}, bf16[416,512]{1,0:T(8,128)(2,1)S(1)}, u32[]{:S(2)}, u32[]{:S(2)}) collective-permute-start(bf16[416,512]{1,0:T(8,128)(2,1)S(1)} %get-tuple-element.35), channel_id=1, source_target_pairs={{0,4},{1,5},{2,6},{3,7},{4,0},{5,1},{6,2},{7,3},{8,12},{9,13},{10,... | collective-permute-start | bytes 1277960 | tf_op jit(solution)/shard_map/ppermute | solution.py:378
  42.9 6.7 %collective-permute-start.3 = (bf16[208,512]{1,0:T(8,128)(2,1)S(1)}, bf16[208,512]{1,0:T(8,128)(2,1)S(1)}, u32[]{:S(2)}, u32[]{:S(2)}) collective-permute-start(bf16[208,512]{1,0:T(8,128)(2,1)S(1)} %get-tuple-element.40), channel_id=1, source_target_pairs={{0,4},{1,5},{2,6},{3,7},{4,0},{5,1},{6,2},{7,3},{8,12},{9,13},{10,... | collective-permute-start | bytes 638984 | tf_op jit(solution)/shard_map/ppermute | solution.py:378
  44.6 6.3 %collective-permute-start.5 = (bf16[208,512]{1,0:T(8,128)(2,1)S(1)}, bf16[208,512]{1,0:T(8,128)(2,1)S(1)}, u32[]{:S(2)}, u32[]{:S(2)}) collective-permute-start(bf16[208,512]{1,0:T(8,128)(2,1)S(1)} %get-tuple-element.45), channel_id=1, source_target_pairs={{0,2},{1,3},{2,0},{3,1},{4,6},{5,7},{6,4},{7,5},{8,10},{9,11},{10,... | collective-permute-start | bytes 638984 | tf_op jit(solution)/shard_map/ppermute | solution.py:378
  50.9 9.7 %collective-permute-start.7 = (bf16[104,512]{1,0:T(8,128)(2,1)S(1)}, bf16[104,512]{1,0:T(8,128)(2,1)S(1)}, u32[]{:S(2)}, u32[]{:S(2)}) collective-permute-start(bf16[104,512]{1,0:T(8,128)(2,1)S(1)} %get-tuple-element.47), channel_id=1, source_target_pairs={{0,8},{1,9},{2,10},{3,11},{4,12},{5,13},{6,14},{7,15},{8,0},{9,1},... | collective-permute-start | bytes 319496 | tf_op jit(solution)/shard_map/ppermute | solution.py:378
  52.4 9.4 %collective-permute-start.6 = (bf16[104,512]{1,0:T(8,128)(2,1)S(1)}, bf16[104,512]{1,0:T(8,128)(2,1)S(1)}, u32[]{:S(2)}, u32[]{:S(2)}) collective-permute-start(bf16[104,512]{1,0:T(8,128)(2,1)S(1)} %get-tuple-element.42), channel_id=1, source_target_pairs={{0,8},{1,9},{2,10},{3,11},{4,12},{5,13},{6,14},{7,15},{8,0},{9,1},... | collective-permute-start | bytes 319496 | tf_op jit(solution)/shard_map/ppermute | solution.py:378
  62.3 10.4 %collective-permute-start.12 = (bf16[104,512]{1,0:T(8,128)(2,1)S(1)}, bf16[104,512]{1,0:T(8,128)(2,1)S(1)}, u32[]{:S(2)}, u32[]{:S(2)}) collective-permute-start(bf16[104,512]{1,0:T(8,128)(2,1)S(1)} %get-tuple-element.49.refs_0_), channel_id=1, source_target_pairs={{0,8},{1,9},{2,10},{3,11},{4,12},{5,13},{6,14},{7,15},{8,0},{9,1},... | collective-permute-start | bytes 319496 | tf_op jit(solution)/shard_map/ppermute | solution.py:378
  62.4 11.5 %collective-permute-start.8 = (bf16[104,512]{1,0:T(8,128)(2,1)S(1)}, bf16[104,512]{1,0:T(8,128)(2,1)S(1)}, u32[]{:S(2)}, u32[]{:S(2)}) collective-permute-start(bf16[104,512]{1,0:T(8,128)(2,1)S(1)} %get-tuple-element.48.refs_0_), channel_id=1, source_target_pairs={{0,8},{1,9},{2,10},{3,11},{4,12},{5,13},{6,14},{7,15},{8,0},{9,1},... | collective-permute-start | bytes 319496 | tf_op jit(solution)/shard_map/ppermute | solution.py:378
  72.7 5.9 %collective-permute-start.13 = (bf16[208,512]{1,0:T(8,128)(2,1)S(1)}, bf16[208,512]{1,0:T(8,128)(2,1)S(1)}, u32[]{:S(2)}, u32[]{:S(2)}) collective-permute-start(bf16[208,512]{1,0:T(8,128)(2,1)S(1)} %shard_map.136.refs_0_), channel_id=1, source_target_pairs={{0,4},{1,5},{2,6},{3,7},{4,0},{5,1},{6,2},{7,3},{8,12},{9,13},{10,... | collective-permute-start | bytes 638984 | tf_op jit(solution)/shard_map/ppermute | solution.py:378
  73.9 7.3 %collective-permute-start.9 = (bf16[208,512]{1,0:T(8,128)(2,1)S(1)}, bf16[208,512]{1,0:T(8,128)(2,1)S(1)}, u32[]{:S(2)}, u32[]{:S(2)}) collective-permute-start(bf16[208,512]{1,0:T(8,128)(2,1)S(1)} %shard_map.133.refs_0_), channel_id=1, source_target_pairs={{0,2},{1,3},{2,0},{3,1},{4,6},{5,7},{6,4},{7,5},{8,10},{9,11},{10,... | collective-permute-start | bytes 638984 | tf_op jit(solution)/shard_map/ppermute | solution.py:378
  78.7 10.3 %collective-permute-start.14 = (bf16[416,512]{1,0:T(8,128)(2,1)S(1)}, bf16[416,512]{1,0:T(8,128)(2,1)S(1)}, u32[]{:S(2)}, u32[]{:S(2)}) collective-permute-start(bf16[416,512]{1,0:T(8,128)(2,1)S(1)} %shard_map.137.refs_0_), channel_id=1, source_target_pairs={{0,2},{1,3},{2,0},{3,1},{4,6},{5,7},{6,4},{7,5},{8,10},{9,11},{10,... | collective-permute-start | bytes 1277960 | tf_op jit(solution)/shard_map/ppermute | solution.py:378
  81.3 8.4 %collective-permute-start.10 = (bf16[416,512]{1,0:T(8,128)(2,1)S(1)}, bf16[416,512]{1,0:T(8,128)(2,1)S(1)}, u32[]{:S(2)}, u32[]{:S(2)}) collective-permute-start(bf16[416,512]{1,0:T(8,128)(2,1)S(1)} %shard_map.134.refs_0_), channel_id=1, source_target_pairs={{0,4},{1,5},{2,6},{3,7},{4,0},{5,1},{6,2},{7,3},{8,12},{9,13},{10,... | collective-permute-start | bytes 1277960 | tf_op jit(solution)/shard_map/ppermute | solution.py:378
  89.1 2.8 %collective-permute-start.15 = (bf16[832,512]{1,0:T(8,128)(2,1)S(1)}, bf16[832,512]{1,0:T(8,128)(2,1)S(1)}, u32[]{:S(2)}, u32[]{:S(2)}) collective-permute-start(bf16[832,512]{1,0:T(8,128)(2,1)S(1)} %shard_map.138.refs_2_), channel_id=1, source_target_pairs={{0,1},{1,0},{2,3},{3,2},{4,5},{5,4},{6,7},{7,6},{8,9},{9,8},{10,11... | collective-permute-start | bytes 2555912 | tf_op jit(solution)/shard_map/ppermute | solution.py:378
  89.7 3.2 %collective-permute-start.11 = (bf16[832,512]{1,0:T(8,128)(2,1)S(1)}, bf16[832,512]{1,0:T(8,128)(2,1)S(1)}, u32[]{:S(2)}, u32[]{:S(2)}) collective-permute-start(bf16[832,512]{1,0:T(8,128)(2,1)S(1)} %shard_map.135.refs_1_), channel_id=1, source_target_pairs={{0,1},{1,0},{2,3},{3,2},{4,5},{5,4},{6,7},{7,6},{8,9},{9,8},{10,11... | collective-permute-start | bytes 2555912 | tf_op jit(solution)/shard_map/ppermute | solution.py:378
  (9 other events, 9.1 us)
